TPU v7x, 256 devices: a whole 4x4x8 slice. The times are simulated.
256 devices in a mesh: section: 8 (over z), expert: 32 (over y, x, core).
Axes of the slice: x: 4, y: 4, z: 8, core: 2. Of those that a mesh axis runs over, the one named last changes fastest.
Arguments:
- hidden_in: bfloat16 [2, 256, 3584], P(None, 'expert'), may hold values from -6 to 6
- layer_gain: float32 [8, 3584], P('section'), may hold values from 0.25 to 1.75
- router: bfloat16 [8, 3584, 8], P('section'), may hold values from -0.09375 to 0.09375
- w_gate: bfloat16 [8, 3584, 16384], P('section', None, 'expert'), may hold values from -0.09375 to 0.09375
- w_up: bfloat16 [8, 3584, 16384], P('section', None, 'expert'), may hold values from -0.09375 to 0.09375
- w_down: bfloat16 [8, 16384, 3584], P('section', 'expert'), may hold values from -0.125 to 0.125
- final_gain: float32 [3584], replicated, may hold values from 0.25 to 1.75
- head: bfloat16 [65536, 3584], P(('section', 'expert')), may hold values from -18.775102 to 18.775102
- routing: int32 [8, 2, 256, 2], P('section', None, 'expert'), may hold values from 0 to 7, all different within a row; in each aligned block of 8 rows (0 to 7, 8 to 15, ..., all dimensions but the last counted through in order) at most 2 rows name the same one
- targets: int32 [2, 256], replicated, may hold values from 0 to 65535
- seq_ids: int32 [2, 256], replicated, may hold values from 0 to 3, never falling along the last dimension, each value on 1 to 128 neighbouring positions
Outputs:
- token_logprob: float32 [2, 256], P(None, 'expert')
- seq_mean: float32 [2, 4], replicated
Inputs may be any that keep to these rules, and one draw needn't show every extreme that they name: `routing`: in each aligned block of 8 tokens (the tokens of one device) a token's 2 experts differ and no expert is named by more than 2 tokens; some expert is named by exactly 2. `seq_ids`: ids never fall along a micro-batch's tokens; each of the 4 ids occurs on 1 to 128 tokens, one on exactly 128.
All inputs are finite; a program needn't handle non-finite values.
Results may differ from a plain program's by a relative error of at most 0.014.
Values may be sent and summed in bfloat16 or wider, within the bound.
A program may use at most 64 MiB of HBM per device.

v0:
```python
import jax
import jax.numpy as jnp
from jax import lax
from jax.sharding import Mesh
from jax.sharding import PartitionSpec as P

SEQS = 4
EXPERT = ("expert_0", "expert_1", "expert_2")
SECTION_EXPERT = ("section", "expert_0", "expert_1", "expert_2")


def shifted(shard, axis, by):
    size = lax.axis_size(axis)
    pairs = [(i, i + by) for i in range(size) if 0 <= i + by < size]
    return lax.ppermute(shard, axis, pairs)


def from_root(shard, axis, root):
    return lax.dynamic_index_in_dim(lax.all_gather(shard, axis), root, 0, keepdims=False)


def collected_together(shard, axis):
    leaves = jax.tree.leaves(shard)
    turns = sorted(range(len(leaves)), key=lambda k: -leaves[k].size)
    width = (1, *leaves[turns[0]].shape)[-1]
    lines = [
        jnp.pad(leaves[k].reshape(-1), (0, -leaves[k].size % width)).reshape(-1, width)
        for k in turns
    ]
    both, at, found = (lax.all_gather(jnp.concatenate(lines), axis), 0, {})
    for k, line in zip(turns, lines):
        piece = both[:, at : at + len(line)].reshape(len(both), -1)
        found[k] = piece[:, : leaves[k].size].reshape(-1, *leaves[k].shape)
        at += len(line)
    numbers = iter(range(len(leaves)))
    return jax.tree.map(lambda _: found[next(numbers)], shard)


def joined_all(shard, axes, combine):
    for axis in axes:
        pieces = collected_together(shard, axis)
        shard = jax.tree.map(lambda part: part[0], pieces)
        for k in range(1, lax.axis_size(axis)):
            shard = combine(shard, jax.tree.map(lambda part: part[k], pieces))
    return shard


def rms_scale(states, gain):
    values = states.astype(jnp.float32)
    factor = lax.rsqrt(jnp.mean(values * values, -1, keepdims=True) + 1e-06)
    return values * factor * gain


def join_stats(first_part, second_part):
    peak = jnp.maximum(first_part[0], second_part[0])
    total = first_part[1] * jnp.exp(first_part[0] - peak) + second_part[1] * jnp.exp(
        second_part[0] - peak
    )
    return (peak, total, first_part[2] + second_part[2])


def body(
    hidden_in, layer_gain, router, w_gate, w_up, w_down, final_gain, head, routing, targets, seq_ids
):
    micro_count, tok_count, model_width = hidden_in.shape
    expert_count = router.shape[2]
    top_count = routing.shape[3]
    sections = lax.axis_size("section")
    members = lax.axis_size(EXPERT)
    section_pos = lax.axis_index("section")
    member_pos = lax.axis_index(EXPERT)
    split_count = members // expert_count
    capacity = min(tok_count, 9 * tok_count * top_count // (8 * expert_count))
    tick_count = micro_count + sections - 1

    def expert_rows(incoming):
        sources, slot_count, width_in = incoming.shape
        flat_rows = incoming.reshape(sources * slot_count, width_in)
        gate_val = jnp.dot(flat_rows, w_gate[0], preferred_element_type=jnp.float32)
        up_val = jnp.dot(flat_rows, w_up[0], preferred_element_type=jnp.float32)
        inner = (jax.nn.silu(gate_val) * up_val).astype(jnp.bfloat16)
        partial_value = jnp.dot(inner, w_down[0], preferred_element_type=jnp.float32).astype(
            jnp.bfloat16
        )
        return lax.all_to_all(
            partial_value.reshape(sources, slot_count, width_in),
            EXPERT,
            split_axis=0,
            concat_axis=0,
            tiled=True,
        )

    def expert_layer(states, micro_pos):
        route_ids = lax.dynamic_index_in_dim(routing[0], micro_pos, 0, keepdims=False)
        normed = rms_scale(states, layer_gain[0]).astype(jnp.bfloat16)
        logits = jnp.dot(normed, router[0], preferred_element_type=jnp.float32)
        chosen = route_ids[:, :, None] == jnp.arange(expert_count, dtype=jnp.int32)[None, None, :]
        affinity = jax.nn.sigmoid(jnp.sum(jnp.where(chosen, logits[:, None, :], 0.0), -1))
        weight = affinity / jnp.sum(affinity, -1, keepdims=True)
        flags = chosen.reshape(tok_count * top_count, expert_count).astype(jnp.int32)
        ranks = jnp.cumsum(flags, 0) - flags
        slot_ids = jnp.sum(ranks * flags, -1).reshape(tok_count, top_count)
        destination = route_ids * capacity + slot_ids
        places = jnp.arange(expert_count * capacity, dtype=jnp.int32)
        table = jnp.any(places[:, None, None] == destination[None], -1).astype(jnp.bfloat16)
        packed = jnp.dot(table, normed, preferred_element_type=jnp.float32).astype(jnp.bfloat16)
        outgoing = jnp.broadcast_to(
            packed.reshape(expert_count, 1, capacity, model_width),
            (expert_count, split_count, capacity, model_width),
        )
        outgoing = outgoing.reshape(members, capacity, model_width)
        returned = expert_rows(
            lax.all_to_all(outgoing, EXPERT, split_axis=0, concat_axis=0, tiled=True)
        )
        summed = jnp.sum(
            returned.reshape(expert_count, split_count, capacity, model_width).astype(jnp.float32),
            1,
        )
        summed = summed.reshape(expert_count * capacity, model_width)
        picked = summed[destination]
        mixed = jnp.sum(weight[:, :, None] * picked, 1)
        return (states.astype(jnp.float32) + 2.5 * mixed).astype(jnp.bfloat16)

    def advance(step, carry):
        arrived, record = carry
        entering = lax.dynamic_index_in_dim(
            hidden_in, jnp.minimum(step, micro_count - 1), 0, keepdims=False
        )
        states = jnp.where(section_pos == 0, entering, arrived)
        micro_pos = jnp.clip(step - section_pos, 0, micro_count - 1)
        result = expert_layer(states, micro_pos)
        finished = step - (sections - 1)
        record_pos = jnp.clip(finished, 0, micro_count - 1)
        keeping = (finished >= 0) & (section_pos == sections - 1)
        previous = lax.dynamic_index_in_dim(record, record_pos, 0, keepdims=False)
        record = lax.dynamic_update_index_in_dim(
            record, jnp.where(keeping, result, previous), record_pos, 0
        )
        arrived = shifted(result, "section", 1)
        return (arrived, record)

    start_rows = jnp.zeros((tok_count, model_width), jnp.bfloat16)
    start_record = jnp.zeros((micro_count, tok_count, model_width), jnp.bfloat16)
    arrived, record = lax.fori_loop(0, tick_count, advance, (start_rows, start_record))
    shared = from_root(record, "section", sections - 1)
    normed = rms_scale(lax.all_gather(shared, EXPERT, axis=1, tiled=True), final_gain).astype(
        jnp.bfloat16
    )
    logits = jnp.einsum("mrd,vd->mrv", normed, head, preferred_element_type=jnp.float32)
    voc_count = head.shape[0]
    vocab_start = (section_pos * members + member_pos) * voc_count
    vocab_ids = vocab_start + jnp.arange(voc_count, dtype=jnp.int32)
    target_hit = targets[:, :, None] == vocab_ids[None, None, :]
    target_part = jnp.sum(jnp.where(target_hit, logits, 0.0), -1)
    local_max = jnp.max(logits, -1)
    local_sum = jnp.sum(jnp.exp(logits - local_max[..., None]), -1)
    peak, total, target_logit = joined_all(
        (local_max, local_sum, target_part), SECTION_EXPERT, join_stats
    )
    logprob = target_logit - (peak + jnp.log(total))
    token_part = lax.dynamic_slice_in_dim(logprob, member_pos * tok_count, tok_count, 1)
    member = seq_ids[:, :, None] == jnp.arange(SEQS, dtype=jnp.int32)[None, None, :]
    sums = jnp.sum(jnp.where(member, logprob[..., None], 0.0), 1)
    counts = jnp.sum(member.astype(jnp.float32), 1)
    return (token_part, sums / counts)


def solution(mesh):
    finer = Mesh(
        mesh.devices.reshape(mesh.shape["section"], 4, 4, 2),
        ("section", "expert_0", "expert_1", "expert_2"),
    )
    placed = (
        P(None, EXPERT, None),
        P("section", None),
        P("section", None, None),
        P("section", None, EXPERT),
        P("section", None, EXPERT),
        P("section", EXPERT, None),
        P(),
        P(SECTION_EXPERT, None),
        P("section", None, EXPERT, None),
        P(),
        P(),
    )
    return jax.shard_map(
        body, mesh=finer, in_specs=placed, out_specs=(P(None, EXPERT), P()), check_vma=False
    )
```

profile of v0, /device:TPU:1, one launch (start us, length us, event | category | flops | bytes accessed | tf_op | source)
XLA Modules:
  0.0 624.2 jit_solution(13239061195931836189)
XLA Ops:
  7.3 469.0 %while.17 = (s32[]{:T(128)}, bf16[8,3584]{1,0:T(8,128)(2,1)S(1)}, bf16[2,8,3584]{2,1,0:T(8,128)(2,1)S(1)}, pred[]{:T(512)}, bf16[2,8,3584]{2,1,0:T(8,128)(2,1)},...) while((s32[]{:T(128)}, bf16[8,3584]{1,0:T(8,128)(2,1)S(1)}, ...), condition=%wide.region_9.10_spmd, body=%wide.region_0.9_spmd.sunk | while | flops 707482304 | bytes 21661588 | solution.py:144
  12.5 8.6 %all-to-all-start = ((bf16[32,2,3584]{2,1,0:T(2,128)(2,1)}), bf16[32,2,3584]{2,1,0:T(2,128)(2,1)S(1)}, u32[]{:S(2)}, u32[]{:S(2)}) async-start(bf16[32,2,3584]{2,1,0:T(2,128)(2,1)} %bitcast.421), calls=%async_computation | async-start | bytes 917504 | tf_op jit(solution)/shard_map/while/body/eval_jaxpr/all_to_all | solution.py:113
  24.1 7.8 %all-to-all-done = bf16[32,2,3584]{2,1,0:T(2,128)(2,1)S(1)} async-done(((bf16[32,2,3584]{2,1,0:T(2,128)(2,1)}), bf16[32,2,3584]{2,1,0:T(2,128)(2,1)S(1)}, u32[]{:S(2)}, u32[]{:S(2)}) %all-to-all-start) | async-done | bytes 458784 | tf_op jit(solution)/shard_map/while/body/eval_jaxpr/all_to_all | solution.py:113
  34.9 4.6 convolution_convert_fusion.5
  44.3 10.9 %all-to-all-done.1 = bf16[32,2,3584]{2,1,0:T(2,128)(2,1)S(1)} async-done(((bf16[32,2,3584]{2,1,0:T(2,128)(2,1)}), bf16[32,2,3584]{2,1,0:T(2,128)(2,1)S(1)}, u32[]{:S(2)}, u32[]{:S(2)}) %all-to-all-start.1) | async-done | bytes 458784 | tf_op jit(solution)/shard_map/while/body/eval_jaxpr/all_to_all | solution.py:85
  66.9 4.7 all-to-all-start
  74.6 7.9 %all-to-all-done = bf16[32,2,3584]{2,1,0:T(2,128)(2,1)S(1)} async-done(((bf16[32,2,3584]{2,1,0:T(2,128)(2,1)}), bf16[32,2,3584]{2,1,0:T(2,128)(2,1)S(1)}, u32[]{:S(2)}, u32[]{:S(2)}) %all-to-all-start) | async-done | bytes 458784 | tf_op jit(solution)/shard_map/while/body/eval_jaxpr/all_to_all | solution.py:113
  85.5 4.6 convolution_convert_fusion.5
  95.0 10.9 %all-to-all-done.1 = bf16[32,2,3584]{2,1,0:T(2,128)(2,1)S(1)} async-done(((bf16[32,2,3584]{2,1,0:T(2,128)(2,1)}), bf16[32,2,3584]{2,1,0:T(2,128)(2,1)S(1)}, u32[]{:S(2)}, u32[]{:S(2)}) %all-to-all-start.1) | async-done | bytes 458784 | tf_op jit(solution)/shard_map/while/body/eval_jaxpr/all_to_all | solution.py:85
  118.0 4.7 all-to-all-start
  125.7 7.9 %all-to-all-done = bf16[32,2,3584]{2,1,0:T(2,128)(2,1)S(1)} async-done(((bf16[32,2,3584]{2,1,0:T(2,128)(2,1)}), bf16[32,2,3584]{2,1,0:T(2,128)(2,1)S(1)}, u32[]{:S(2)}, u32[]{:S(2)}) %all-to-all-start) | async-done | bytes 458784 | tf_op jit(solution)/shard_map/while/body/eval_jaxpr/all_to_all | solution.py:113
  136.5 4.6 convolution_convert_fusion.5
  146.0 10.9 %all-to-all-done.1 = bf16[32,2,3584]{2,1,0:T(2,128)(2,1)S(1)} async-done(((bf16[32,2,3584]{2,1,0:T(2,128)(2,1)}), bf16[32,2,3584]{2,1,0:T(2,128)(2,1)S(1)}, u32[]{:S(2)}, u32[]{:S(2)}) %all-to-all-start.1) | async-done | bytes 458784 | tf_op jit(solution)/shard_map/while/body/eval_jaxpr/all_to_all | solution.py:85
  169.0 4.7 all-to-all-start
  176.8 7.9 %all-to-all-done = bf16[32,2,3584]{2,1,0:T(2,128)(2,1)S(1)} async-done(((bf16[32,2,3584]{2,1,0:T(2,128)(2,1)}), bf16[32,2,3584]{2,1,0:T(2,128)(2,1)S(1)}, u32[]{:S(2)}, u32[]{:S(2)}) %all-to-all-start) | async-done | bytes 458784 | tf_op jit(solution)/shard_map/while/body/eval_jaxpr/all_to_all | solution.py:113
  187.6 4.6 convolution_convert_fusion.5
  197.1 10.9 %all-to-all-done.1 = bf16[32,2,3584]{2,1,0:T(2,128)(2,1)S(1)} async-done(((bf16[32,2,3584]{2,1,0:T(2,128)(2,1)}), bf16[32,2,3584]{2,1,0:T(2,128)(2,1)S(1)}, u32[]{:S(2)}, u32[]{:S(2)}) %all-to-all-start.1) | async-done | bytes 458784 | tf_op jit(solution)/shard_map/while/body/eval_jaxpr/all_to_all | solution.py:85
  220.1 4.7 all-to-all-start
  227.8 7.9 %all-to-all-done = bf16[32,2,3584]{2,1,0:T(2,128)(2,1)S(1)} async-done(((bf16[32,2,3584]{2,1,0:T(2,128)(2,1)}), bf16[32,2,3584]{2,1,0:T(2,128)(2,1)S(1)}, u32[]{:S(2)}, u32[]{:S(2)}) %all-to-all-start) | async-done | bytes 458784 | tf_op jit(solution)/shard_map/while/body/eval_jaxpr/all_to_all | solution.py:113
  238.7 4.6 convolution_convert_fusion.5
  248.1 10.9 %all-to-all-done.1 = bf16[32,2,3584]{2,1,0:T(2,128)(2,1)S(1)} async-done(((bf16[32,2,3584]{2,1,0:T(2,128)(2,1)}), bf16[32,2,3584]{2,1,0:T(2,128)(2,1)S(1)}, u32[]{:S(2)}, u32[]{:S(2)}) %all-to-all-start.1) | async-done | bytes 458784 | tf_op jit(solution)/shard_map/while/body/eval_jaxpr/all_to_all | solution.py:85
  260.8 5.1 collective-permute-start
  272.3 4.7 all-to-all-start
  280.0 7.9 %all-to-all-done = bf16[32,2,3584]{2,1,0:T(2,128)(2,1)S(1)} async-done(((bf16[32,2,3584]{2,1,0:T(2,128)(2,1)}), bf16[32,2,3584]{2,1,0:T(2,128)(2,1)S(1)}, u32[]{:S(2)}, u32[]{:S(2)}) %all-to-all-start) | async-done | bytes 458784 | tf_op jit(solution)/shard_map/while/body/eval_jaxpr/all_to_all | solution.py:113
  290.9 4.6 convolution_convert_fusion.5
  300.3 10.9 %all-to-all-done.1 = bf16[32,2,3584]{2,1,0:T(2,128)(2,1)S(1)} async-done(((bf16[32,2,3584]{2,1,0:T(2,128)(2,1)}), bf16[32,2,3584]{2,1,0:T(2,128)(2,1)S(1)}, u32[]{:S(2)}, u32[]{:S(2)}) %all-to-all-start.1) | async-done | bytes 458784 | tf_op jit(solution)/shard_map/while/body/eval_jaxpr/all_to_all | solution.py:85
  313.0 5.2 collective-permute-start
  324.5 4.7 all-to-all-start
  332.3 7.9 %all-to-all-done = bf16[32,2,3584]{2,1,0:T(2,128)(2,1)S(1)} async-done(((bf16[32,2,3584]{2,1,0:T(2,128)(2,1)}), bf16[32,2,3584]{2,1,0:T(2,128)(2,1)S(1)}, u32[]{:S(2)}, u32[]{:S(2)}) %all-to-all-start) | async-done | bytes 458784 | tf_op jit(solution)/shard_map/while/body/eval_jaxpr/all_to_all | solution.py:113
  343.1 4.6 convolution_convert_fusion.5
  352.6 10.9 %all-to-all-done.1 = bf16[32,2,3584]{2,1,0:T(2,128)(2,1)S(1)} async-done(((bf16[32,2,3584]{2,1,0:T(2,128)(2,1)}), bf16[32,2,3584]{2,1,0:T(2,128)(2,1)S(1)}, u32[]{:S(2)}, u32[]{:S(2)}) %all-to-all-start.1) | async-done | bytes 458784 | tf_op jit(solution)/shard_map/while/body/eval_jaxpr/all_to_all | solution.py:85
  365.3 5.2 collective-permute-start
  376.8 4.7 all-to-all-start
  384.6 7.9 %all-to-all-done = bf16[32,2,3584]{2,1,0:T(2,128)(2,1)S(1)} async-done(((bf16[32,2,3584]{2,1,0:T(2,128)(2,1)}), bf16[32,2,3584]{2,1,0:T(2,128)(2,1)S(1)}, u32[]{:S(2)}, u32[]{:S(2)}) %all-to-all-start) | async-done | bytes 458784 | tf_op jit(solution)/shard_map/while/body/eval_jaxpr/all_to_all | solution.py:113
  395.4 4.6 convolution_convert_fusion.5
  404.9 10.9 %all-to-all-done.1 = bf16[32,2,3584]{2,1,0:T(2,128)(2,1)S(1)} async-done(((bf16[32,2,3584]{2,1,0:T(2,128)(2,1)}), bf16[32,2,3584]{2,1,0:T(2,128)(2,1)S(1)}, u32[]{:S(2)}, u32[]{:S(2)}) %all-to-all-start.1) | async-done | bytes 458784 | tf_op jit(solution)/shard_map/while/body/eval_jaxpr/all_to_all | solution.py:85
  417.5 5.2 collective-permute-start
  429.1 4.7 all-to-all-start
  436.8 7.9 %all-to-all-done = bf16[32,2,3584]{2,1,0:T(2,128)(2,1)S(1)} async-done(((bf16[32,2,3584]{2,1,0:T(2,128)(2,1)}), bf16[32,2,3584]{2,1,0:T(2,128)(2,1)S(1)}, u32[]{:S(2)}, u32[]{:S(2)}) %all-to-all-start) | async-done | bytes 458784 | tf_op jit(solution)/shard_map/while/body/eval_jaxpr/all_to_all | solution.py:113
  447.7 4.6 convolution_convert_fusion.5
  457.1 10.9 %all-to-all-done.1 = bf16[32,2,3584]{2,1,0:T(2,128)(2,1)S(1)} async-done(((bf16[32,2,3584]{2,1,0:T(2,128)(2,1)}), bf16[32,2,3584]{2,1,0:T(2,128)(2,1)S(1)}, u32[]{:S(2)}, u32[]{:S(2)}) %all-to-all-start.1) | async-done | bytes 458784 | tf_op jit(solution)/shard_map/while/body/eval_jaxpr/all_to_all | solution.py:85
  469.8 5.2 collective-permute-start
  476.2 29.0 %all-gather = bf16[16,8,3584]{2,1,0:T(8,128)(2,1)S(1)} all-gather(bf16[2,8,3584]{2,1,0:T(8,128)(2,1)S(1)} %get-tuple-element.277), channel_id=2, replica_groups=mesh['section'=8,'expert_0'=4,'expert_1'=4,'expert_2'=2] {'section'}, dimensions={0}, use_global_device_ids=true | all-gather | bytes 1032192 | tf_op jit(solution)/shard_map/all_gather | solution.py:19
  505.9 53.5 %all-gather.13.cloned.1.call-done = bf16[2,256,3584]{2,1,0:T(8,128)(2,1)} async-done(((bf16[2,8,3584]{2,1,0:T(8,128)(2,1)}), bf16[2,256,3584]{2,1,0:T(8,128)(2,1)}) %all-gather.13.cloned.1.call-update) | async-done | bytes 3670032 | tf_op jit(solution)/shard_map/all_gather | solution.py:146
  564.2 19.7 %all-gather.7 = f32[8,6,256]{2,1,0:T(8,128)S(1)} all-gather(f32[1,6,256]{2,1,0:T(8,128)S(1)} %maximum_bitcast_fusion), channel_id=4, replica_groups=mesh['section'=8,'expert_0'=4,'expert_1'=4,'expert_2'=2] {'section'}, dimensions={0}, use_global_device_ids=true | all-gather | bytes 55296 | tf_op jit(solution)/shard_map/all_gather | solution.py:30
  583.9 9.3 %all-gather.8 = f32[4,6,256]{2,1,0:T(8,128)S(1)} all-gather(f32[1,6,256]{2,1,0:T(8,128)S(1)} %maximum_bitcast_fusion.1), channel_id=5, replica_groups=mesh['section'=8,'expert_0'=4,'expert_1'=4,'expert_2'=2] {'expert_0'}, dimensions={0}, use_global_device_ids=true | all-gather | bytes 30720 | tf_op jit(solution)/shard_map/all_gather | solution.py:30
  593.3 9.0 %all-gather.9 = f32[4,6,256]{2,1,0:T(8,128)S(1)} all-gather(f32[1,6,256]{2,1,0:T(8,128)S(1)} %maximum_bitcast_fusion.2), channel_id=6, replica_groups=mesh['section'=8,'expert_0'=4,'expert_1'=4,'expert_2'=2] {'expert_1'}, dimensions={0}, use_global_device_ids=true | all-gather | bytes 30720 | tf_op jit(solution)/shard_map/all_gather | solution.py:30
  602.4 13.6 %all-gather.10 = f32[2,6,256]{2,1,0:T(8,128)S(1)} all-gather(f32[1,6,256]{2,1,0:T(8,128)S(1)} %maximum_bitcast_fusion.3), channel_id=7, replica_groups=mesh['section'=8,'expert_0'=4,'expert_1'=4,'expert_2'=2] {'expert_2'}, dimensions={0}, use_global_device_ids=true | all-gather | bytes 18432 | tf_op jit(solution)/shard_map/all_gather | solution.py:30
  (398 shorter events, 192.1 us)
Async XLA Ops:
  7.2 555.3 %copy-start = (bf16[256,3584]{1,0:T(8,128)(2,1)S(1)}, bf16[256,3584]{1,0:T(8,128)(2,1)}, u32[]{:S(2)}) copy-start(bf16[256,3584]{1,0:T(8,128)(2,1)} %param.20) | copy-start | bytes 5505028
  7.2 552.3 %all-gather.13.cloned.1.call-start = ((), (), s32[]{:S(2)}) async-start(), calls=%async_computation.2 | async-start | bytes 3784704 | tf_op jit(solution)/shard_map/all_gather | solution.py:146
  12.5 19.4 %all-to-all-start = ((bf16[32,2,3584]{2,1,0:T(2,128)(2,1)}), bf16[32,2,3584]{2,1,0:T(2,128)(2,1)S(1)}, u32[]{:S(2)}, u32[]{:S(2)}) async-start(bf16[32,2,3584]{2,1,0:T(2,128)(2,1)} %bitcast.421), calls=%async_computation | async-start | bytes 917504 | tf_op jit(solution)/shard_map/while/body/eval_jaxpr/all_to_all | solution.py:113
  40.4 14.8 %all-to-all-start.1 = ((bf16[32,2,3584]{2,1,0:T(2,128)(2,1)}), bf16[32,2,3584]{2,1,0:T(2,128)(2,1)S(1)}, u32[]{:S(2)}, u32[]{:S(2)}) async-start(bf16[32,2,3584]{2,1,0:T(2,128)(2,1)} %reshape.321), calls=%async_computation.1 | async-start | bytes 917504 | tf_op jit(solution)/shard_map/while/body/eval_jaxpr/all_to_all | solution.py:85
  57.0 4.8 collective-permute-start
  66.9 15.6 %all-to-all-start = ((bf16[32,2,3584]{2,1,0:T(2,128)(2,1)}), bf16[32,2,3584]{2,1,0:T(2,128)(2,1)S(1)}, u32[]{:S(2)}, u32[]{:S(2)}) async-start(bf16[32,2,3584]{2,1,0:T(2,128)(2,1)} %bitcast.421), calls=%async_computation | async-start | bytes 917504 | tf_op jit(solution)/shard_map/while/body/eval_jaxpr/all_to_all | solution.py:113
  91.1 14.8 %all-to-all-start.1 = ((bf16[32,2,3584]{2,1,0:T(2,128)(2,1)}), bf16[32,2,3584]{2,1,0:T(2,128)(2,1)S(1)}, u32[]{:S(2)}, u32[]{:S(2)}) async-start(bf16[32,2,3584]{2,1,0:T(2,128)(2,1)} %reshape.321), calls=%async_computation.1 | async-start | bytes 917504 | tf_op jit(solution)/shard_map/while/body/eval_jaxpr/all_to_all | solution.py:85
  107.6 5.2 collective-permute-start
  118.0 15.6 %all-to-all-start = ((bf16[32,2,3584]{2,1,0:T(2,128)(2,1)}), bf16[32,2,3584]{2,1,0:T(2,128)(2,1)S(1)}, u32[]{:S(2)}, u32[]{:S(2)}) async-start(bf16[32,2,3584]{2,1,0:T(2,128)(2,1)} %bitcast.421), calls=%async_computation | async-start | bytes 917504 | tf_op jit(solution)/shard_map/while/body/eval_jaxpr/all_to_all | solution.py:113
  142.1 14.8 %all-to-all-start.1 = ((bf16[32,2,3584]{2,1,0:T(2,128)(2,1)}), bf16[32,2,3584]{2,1,0:T(2,128)(2,1)S(1)}, u32[]{:S(2)}, u32[]{:S(2)}) async-start(bf16[32,2,3584]{2,1,0:T(2,128)(2,1)} %reshape.321), calls=%async_computation.1 | async-start | bytes 917504 | tf_op jit(solution)/shard_map/while/body/eval_jaxpr/all_to_all | solution.py:85
  158.7 5.2 collective-permute-start
  169.0 15.6 %all-to-all-start = ((bf16[32,2,3584]{2,1,0:T(2,128)(2,1)}), bf16[32,2,3584]{2,1,0:T(2,128)(2,1)S(1)}, u32[]{:S(2)}, u32[]{:S(2)}) async-start(bf16[32,2,3584]{2,1,0:T(2,128)(2,1)} %bitcast.421), calls=%async_computation | async-start | bytes 917504 | tf_op jit(solution)/shard_map/while/body/eval_jaxpr/all_to_all | solution.py:113
  193.2 14.8 %all-to-all-start.1 = ((bf16[32,2,3584]{2,1,0:T(2,128)(2,1)}), bf16[32,2,3584]{2,1,0:T(2,128)(2,1)S(1)}, u32[]{:S(2)}, u32[]{:S(2)}) async-start(bf16[32,2,3584]{2,1,0:T(2,128)(2,1)} %reshape.321), calls=%async_computation.1 | async-start | bytes 917504 | tf_op jit(solution)/shard_map/while/body/eval_jaxpr/all_to_all | solution.py:85
  209.7 5.2 collective-permute-start
  220.1 15.6 %all-to-all-start = ((bf16[32,2,3584]{2,1,0:T(2,128)(2,1)}), bf16[32,2,3584]{2,1,0:T(2,128)(2,1)S(1)}, u32[]{:S(2)}, u32[]{:S(2)}) async-start(bf16[32,2,3584]{2,1,0:T(2,128)(2,1)} %bitcast.421), calls=%async_computation | async-start | bytes 917504 | tf_op jit(solution)/shard_map/while/body/eval_jaxpr/all_to_all | solution.py:113
  244.2 14.8 %all-to-all-start.1 = ((bf16[32,2,3584]{2,1,0:T(2,128)(2,1)}), bf16[32,2,3584]{2,1,0:T(2,128)(2,1)S(1)}, u32[]{:S(2)}, u32[]{:S(2)}) async-start(bf16[32,2,3584]{2,1,0:T(2,128)(2,1)} %reshape.321), calls=%async_computation.1 | async-start | bytes 917504 | tf_op jit(solution)/shard_map/while/body/eval_jaxpr/all_to_all | solution.py:85
  260.8 6.3 %collective-permute-start = (bf16[8,3584]{1,0:T(8,128)(2,1)S(1)}, bf16[8,3584]{1,0:T(8,128)(2,1)S(1)}, u32[]{:S(2)}, u32[]{:S(2)}) collective-permute-start(bf16[8,3584]{1,0:T(8,128)(2,1)S(1)} %get-tuple-element.405), channel_id=1, source_target_pairs={{0,32},{32,64},{64,96},{96,128},{128,160},{160,192},{192,224},{1,3... | collective-permute-start | bytes 172040 | tf_op jit(solution)/shard_map/while/body/eval_jaxpr/ppermute | solution.py:15
  272.3 15.6 %all-to-all-start = ((bf16[32,2,3584]{2,1,0:T(2,128)(2,1)}), bf16[32,2,3584]{2,1,0:T(2,128)(2,1)S(1)}, u32[]{:S(2)}, u32[]{:S(2)}) async-start(bf16[32,2,3584]{2,1,0:T(2,128)(2,1)} %bitcast.421), calls=%async_computation | async-start | bytes 917504 | tf_op jit(solution)/shard_map/while/body/eval_jaxpr/all_to_all | solution.py:113
  296.4 14.8 %all-to-all-start.1 = ((bf16[32,2,3584]{2,1,0:T(2,128)(2,1)}), bf16[32,2,3584]{2,1,0:T(2,128)(2,1)S(1)}, u32[]{:S(2)}, u32[]{:S(2)}) async-start(bf16[32,2,3584]{2,1,0:T(2,128)(2,1)} %reshape.321), calls=%async_computation.1 | async-start | bytes 917504 | tf_op jit(solution)/shard_map/while/body/eval_jaxpr/all_to_all | solution.py:85
  313.0 6.4 %collective-permute-start = (bf16[8,3584]{1,0:T(8,128)(2,1)S(1)}, bf16[8,3584]{1,0:T(8,128)(2,1)S(1)}, u32[]{:S(2)}, u32[]{:S(2)}) collective-permute-start(bf16[8,3584]{1,0:T(8,128)(2,1)S(1)} %get-tuple-element.405), channel_id=1, source_target_pairs={{0,32},{32,64},{64,96},{96,128},{128,160},{160,192},{192,224},{1,3... | collective-permute-start | bytes 172040 | tf_op jit(solution)/shard_map/while/body/eval_jaxpr/ppermute | solution.py:15
  324.5 15.6 %all-to-all-start = ((bf16[32,2,3584]{2,1,0:T(2,128)(2,1)}), bf16[32,2,3584]{2,1,0:T(2,128)(2,1)S(1)}, u32[]{:S(2)}, u32[]{:S(2)}) async-start(bf16[32,2,3584]{2,1,0:T(2,128)(2,1)} %bitcast.421), calls=%async_computation | async-start | bytes 917504 | tf_op jit(solution)/shard_map/while/body/eval_jaxpr/all_to_all | solution.py:113
  348.7 14.8 %all-to-all-start.1 = ((bf16[32,2,3584]{2,1,0:T(2,128)(2,1)}), bf16[32,2,3584]{2,1,0:T(2,128)(2,1)S(1)}, u32[]{:S(2)}, u32[]{:S(2)}) async-start(bf16[32,2,3584]{2,1,0:T(2,128)(2,1)} %reshape.321), calls=%async_computation.1 | async-start | bytes 917504 | tf_op jit(solution)/shard_map/while/body/eval_jaxpr/all_to_all | solution.py:85
  365.3 6.4 %collective-permute-start = (bf16[8,3584]{1,0:T(8,128)(2,1)S(1)}, bf16[8,3584]{1,0:T(8,128)(2,1)S(1)}, u32[]{:S(2)}, u32[]{:S(2)}) collective-permute-start(bf16[8,3584]{1,0:T(8,128)(2,1)S(1)} %get-tuple-element.405), channel_id=1, source_target_pairs={{0,32},{32,64},{64,96},{96,128},{128,160},{160,192},{192,224},{1,3... | collective-permute-start | bytes 172040 | tf_op jit(solution)/shard_map/while/body/eval_jaxpr/ppermute | solution.py:15
  376.8 15.6 %all-to-all-start = ((bf16[32,2,3584]{2,1,0:T(2,128)(2,1)}), bf16[32,2,3584]{2,1,0:T(2,128)(2,1)S(1)}, u32[]{:S(2)}, u32[]{:S(2)}) async-start(bf16[32,2,3584]{2,1,0:T(2,128)(2,1)} %bitcast.421), calls=%async_computation | async-start | bytes 917504 | tf_op jit(solution)/shard_map/while/body/eval_jaxpr/all_to_all | solution.py:113
  401.0 14.8 %all-to-all-start.1 = ((bf16[32,2,3584]{2,1,0:T(2,128)(2,1)}), bf16[32,2,3584]{2,1,0:T(2,128)(2,1)S(1)}, u32[]{:S(2)}, u32[]{:S(2)}) async-start(bf16[32,2,3584]{2,1,0:T(2,128)(2,1)} %reshape.321), calls=%async_computation.1 | async-start | bytes 917504 | tf_op jit(solution)/shard_map/while/body/eval_jaxpr/all_to_all | solution.py:85
  417.5 6.4 %collective-permute-start = (bf16[8,3584]{1,0:T(8,128)(2,1)S(1)}, bf16[8,3584]{1,0:T(8,128)(2,1)S(1)}, u32[]{:S(2)}, u32[]{:S(2)}) collective-permute-start(bf16[8,3584]{1,0:T(8,128)(2,1)S(1)} %get-tuple-element.405), channel_id=1, source_target_pairs={{0,32},{32,64},{64,96},{96,128},{128,160},{160,192},{192,224},{1,3... | collective-permute-start | bytes 172040 | tf_op jit(solution)/shard_map/while/body/eval_jaxpr/ppermute | solution.py:15
  429.1 15.6 %all-to-all-start = ((bf16[32,2,3584]{2,1,0:T(2,128)(2,1)}), bf16[32,2,3584]{2,1,0:T(2,128)(2,1)S(1)}, u32[]{:S(2)}, u32[]{:S(2)}) async-start(bf16[32,2,3584]{2,1,0:T(2,128)(2,1)} %bitcast.421), calls=%async_computation | async-start | bytes 917504 | tf_op jit(solution)/shard_map/while/body/eval_jaxpr/all_to_all | solution.py:113
  453.2 14.8 %all-to-all-start.1 = ((bf16[32,2,3584]{2,1,0:T(2,128)(2,1)}), bf16[32,2,3584]{2,1,0:T(2,128)(2,1)S(1)}, u32[]{:S(2)}, u32[]{:S(2)}) async-start(bf16[32,2,3584]{2,1,0:T(2,128)(2,1)} %reshape.321), calls=%async_computation.1 | async-start | bytes 917504 | tf_op jit(solution)/shard_map/while/body/eval_jaxpr/all_to_all | solution.py:85
  469.8 6.4 %collective-permute-start = (bf16[8,3584]{1,0:T(8,128)(2,1)S(1)}, bf16[8,3584]{1,0:T(8,128)(2,1)S(1)}, u32[]{:S(2)}, u32[]{:S(2)}) collective-permute-start(bf16[8,3584]{1,0:T(8,128)(2,1)S(1)} %get-tuple-element.405), channel_id=1, source_target_pairs={{0,32},{32,64},{64,96},{96,128},{128,160},{160,192},{192,224},{1,3... | collective-permute-start | bytes 172040 | tf_op jit(solution)/shard_map/while/body/eval_jaxpr/ppermute | solution.py:15
  476.2 86.3 %copy-start.4 = (f32[3584]{0:T(1024)S(1)}, f32[3584]{0:T(1024)}, u32[]{:S(2)}) copy-start(f32[3584]{0:T(1024)} %param.19) | copy-start | bytes 43012
  559.5 3.1 copy-start.1
  562.6 1.4 copy-start.2
  562.6 53.4 %copy-start.3 = (s32[2,256]{1,0:T(2,128)S(1)}, s32[2,256]{1,0:T(2,128)}, u32[]{:S(2)}) copy-start(s32[2,256]{1,0:T(2,128)} %param.23) | copy-start | bytes 6148
Sparse Core Ops, SparseCore 0:
  506.0 53.3 all-gather.12
where the time goes:
time: 628 us; the launch traced here: 624 us
  waiting for transfers between devices  233 us (37%)
  starting transfers between devices  123 us (20%)
  blocking collectives  80.7 us (13%)
  matrix products  79.2 us (13%)
  local copies, waits for them, and re-layouts  48.4 us (8%)
  other arithmetic  44.5 us (7%)
  between operations  14.2 us (2%)
    all_to_all x9, waiting for transfers between devices, expert_rows(): lax.all_to_all(partial_value.reshape(sources, slot_count, width_in), EXPE...  97.9 us
    all_to_all x9, waiting for transfers between devices, expert_layer(): lax.all_to_all(outgoing, EXPERT, split_axis=0, concat_axis=0, tiled=True)  70.9 us
    all_gather x1, waiting for transfers between devices, body(): lax.all_gather(shared, EXPERT, axis=1, tiled=True)  53.5 us
    all_gather x4, blocking collectives, collected_together(): both, at, found = (lax.all_gather(jnp.concatenate(lines), axis), 0, {})  51.6 us
    all_to_all x9, starting transfers between devices, expert_layer(): lax.all_to_all(outgoing, EXPERT, split_axis=0, concat_axis=0, tiled=True)  46.4 us
    dot_general x9, matrix products, expert_rows(): jnp.dot(inner, w_down[0], preferred_element_type=jnp.float32)  41.5 us
    ppermute x9, starting transfers between devices, shifted(): return lax.ppermute(shard, axis, pairs)  41.3 us
    all_to_all x9, starting transfers between devices, expert_rows(): lax.all_to_all(partial_value.reshape(sources, slot_count, width_in), EXPE...  34.9 us
  transfers between devices with their start and end apart: 28, of which 28 were waited for; matrix products, arithmetic and copies ran while one was open for 4% of the time, Pallas kernels for 0%

commit v1 on v0

v1 whole, which is shorter than its diff:
```python
import jax
import jax.numpy as jnp
from jax import lax
from jax.experimental import pallas as pl
from jax.experimental.pallas import tpu as pltpu
from jax.sharding import PartitionSpec as P

SEQS = 4
CHIPS = 16
F32, BF16, I32 = jnp.float32, jnp.bfloat16, jnp.int32
MESH = pl.DeviceIdType.MESH


def iota(shape, axis):
    return lax.broadcasted_iota(I32, shape, axis)


def rms_scale(states, gain):
    values = states.astype(F32)
    factor = lax.rsqrt(jnp.mean(values * values, -1, keepdims=True) + 1e-06)
    return values * factor * gain


def layers_kernel(
    hidden, gain, router, routes, last_gain, wanted, own_ids, all_ids, gate_hbm, up_hbm, down_hbm, head_hbm,
    token_out, mean_out,
    gate, up, down, head, head_other, gathered, stat_out, stat_in, plane_out, plane_in, seq_out, seq_in, states, packed, mine, other, rows, inner, part, away, back, summed, ret, leaving,
    weight_sem, disp_send, disp_recv, pair_send, pair_recv, half_send, half_recv, ret_send, ret_recv,
    hop_send, hop_recv, head_send, head_recv, cast_send, cast_recv, all_send, all_recv, stat_send, stat_recv,
    plane_send, plane_recv, seq_send, seq_recv,
):
    micro_count, tok_count, width = hidden.shape
    section, member = lax.axis_index("section"), lax.axis_index("expert")
    sections, members = lax.axis_size("section"), lax.axis_size("expert")
    last = sections - 1
    chip, core = member // 2, member % 2
    partner = member + 1 - 2 * core

    loads = [
        pltpu.make_async_copy(source, target, weight_sem.at[k])
        for k, (source, target) in enumerate(((gate_hbm, gate), (up_hbm, up), (down_hbm, down), (head_hbm, head)))
    ]
    for load in loads:
        load.start()

    barrier = pltpu.get_barrier_semaphore()
    for step in range(1, members):
        peer = (member + step) % members
        pl.semaphore_signal(barrier, inc=1, device_id={"expert": peer}, device_id_type=MESH)
    for step in range(1, sections):
        pl.semaphore_signal(
            barrier, inc=1, device_id={"section": (section + step) % sections}, device_id_type=MESH
        )
    pl.semaphore_wait(barrier, members + sections - 2)

    def remote(source, target, send, recv, **where):
        return pltpu.make_async_remote_copy(
            src_ref=source, dst_ref=target, send_sem=send, recv_sem=recv,
            device_id=where, device_id_type=MESH,
        )

    def dispatch(m, step):
        to = (chip + step) % CHIPS
        return remote(
            packed.at[m, to // 2], mine.at[m, chip], disp_send.at[m, step], disp_recv.at[m, chip],
            expert=to * 2 + core,
        )

    def dispatched(m, step):
        source = (chip + step) % CHIPS
        return remote(
            packed.at[m, 0], mine.at[m, source], disp_send.at[m, step], disp_recv.at[m, source],
            expert=partner,
        )

    def giving(m, step):
        to = (chip + step) % CHIPS
        return remote(
            summed.at[m, to], ret.at[m, chip], ret_send.at[m, step], ret_recv.at[m, chip],
            expert=to * 2 + core,
        )

    def given(m, step):
        source = (chip + step) % CHIPS
        return remote(
            summed.at[m, 0], ret.at[m, source], ret_send.at[m, step], ret_recv.at[m, source],
            expert=partner,
        )

    def pair(m):
        return remote(mine.at[m], other.at[m], pair_send.at[m], pair_recv.at[m], expert=partner)

    def halves(m):
        return remote(away.at[m], back.at[m], half_send.at[m], half_recv.at[m], expert=partner)

    def hop(m):
        return remote(
            leaving.at[m], states.at[m], hop_send.at[m], hop_recv.at[m],
            section=(section + 1) % sections,
        )

    head_swap = remote(head_hbm, head_other, head_send, head_recv, expert=partner)

    def cast(m, step):
        return remote(
            gathered.at[m, chip], gathered.at[m, chip], cast_send.at[m, step], cast_recv.at[m],
            section=(section + step) % sections,
        )

    def gather(m, step):
        return remote(
            gathered.at[m, chip], gathered.at[m, chip], all_send.at[m, step], all_recv.at[m, chip],
            expert=(chip + step) % CHIPS * 2 + core,
        )

    def arriving(m, step):
        source = (chip + step) % CHIPS
        return remote(
            gathered.at[m, source], gathered.at[m, source], all_send.at[m, step], all_recv.at[m, source],
            expert=partner,
        )

    def stat_to(m, step):
        to = (chip + step) % CHIPS
        return remote(
            stat_out.at[m, to], stat_in.at[m, chip], stat_send.at[m, step], stat_recv.at[m, chip],
            expert=to * 2 + core,
        )

    def stat_from(m, step):
        source = (chip + step) % CHIPS
        return remote(
            stat_out.at[m, source], stat_in.at[m, source], stat_send.at[m, step], stat_recv.at[m, source],
            expert=partner,
        )

    def plane_to(m, step):
        return remote(
            plane_out.at[m], plane_in.at[m, section], plane_send.at[m, step], plane_recv.at[m, section],
            section=(section + step) % sections,
        )

    def plane_from(m, step):
        source = (section + step) % sections
        return remote(
            plane_out.at[m], plane_in.at[m, source], plane_send.at[m, step], plane_recv.at[m, source],
            section=source,
        )

    def seq_to(step):
        return remote(
            seq_out, seq_in.at[member], seq_send.at[step], seq_recv.at[member],
            expert=(member + step) % members,
        )

    def seq_from(step):
        source = (member + step) % members
        return remote(seq_out, seq_in.at[source], seq_send.at[step], seq_recv.at[source], expert=source)

    @pl.when(section > 0)
    def _():
        head_swap.start()

    before = (iota((tok_count, tok_count), 0) < iota((tok_count, tok_count), 1)).astype(BF16)

    for m in range(micro_count):
        route = routes[m]
        first, second = route[0:1, :], route[1:2, :]

        def slots(count, shift):
            place = iota((count, tok_count), 0)
            expert = lax.shift_right_logical(place, shift)
            hit = ((expert == first) | (expert == second)).astype(F32)
            rank = jnp.dot(hit.astype(BF16), before, preferred_element_type=F32)
            return expert, jnp.where(rank == (place & 1).astype(F32), hit, 0.0)

        _, table = slots(16, 1)
        expert32, held32 = slots(32, 2)

        @pl.when(section == 0)
        def _():
            states[m] = hidden[m]

        @pl.when(section > 0)
        def _():
            hop(m).wait_recv()

        normed = rms_scale(states[m], gain[...]).astype(BF16)
        chosen = jnp.dot(table.astype(BF16), normed, preferred_element_type=F32).astype(BF16)
        packed[m] = chosen.reshape(8, 2, width)
        for step in range(1, CHIPS):
            dispatch(m, step).start()
        mine[m, chip] = packed[m, chip // 2]

        logits = lax.dot_general(router[...], normed, (((1,), (1,)), ((), ())), preferred_element_type=F32)
        row8 = iota((8, tok_count), 0)
        affinity = [
            jax.nn.sigmoid(jnp.sum(jnp.where(row8 == pick, logits, 0.0), 0, keepdims=True))
            for pick in (first, second)
        ]
        total = affinity[0] + affinity[1]
        weight = held32 * jnp.where(
            expert32 == first, affinity[0] / total, jnp.where(expert32 == second, affinity[1] / total, 0.0)
        )

        for step in range(1, CHIPS):
            dispatched(m, step).wait_recv()
        pair(m).start()
        rows[0:32] = mine[m].reshape(32, width)
        if m == 0:
            for load in loads[:3]:
                load.wait()
        pair(m).wait_recv()
        rows[32:64] = other[m].reshape(32, width)

        @pl.loop(0, 2)
        def _(j):
            span = pl.ds(pl.multiple_of(j * 256, 256), 256)
            gate_val = jnp.dot(rows[...], gate[:, span], preferred_element_type=F32)
            up_val = jnp.dot(rows[...], up[:, span], preferred_element_type=F32)
            inner[:, span] = (jax.nn.silu(gate_val) * up_val).astype(BF16)

        @pl.loop(0, 7)
        def _(j):
            span = pl.ds(pl.multiple_of(j * 512, 512), 512)
            result = jnp.dot(inner[...], down[:, span], preferred_element_type=F32)
            part[:, span] = result[0:32]
            away[m, :, :, span] = result[32:64].astype(BF16).reshape(CHIPS, 2, 512)

        halves(m).start()
        halves(m).wait_recv()
        summed[m] = (part[...] + back[m].reshape(32, width).astype(F32)).astype(BF16).reshape(CHIPS, 2, width)
        for step in range(1, CHIPS):
            giving(m, step).start()
        if m == 1:

            @pl.when(section == last)
            def _():
                for step in range(1, CHIPS):
                    gather(0, step).start()

        ret[m, chip] = summed[m, chip]

        high = weight.astype(BF16)
        middle = (weight - high.astype(F32)).astype(BF16)
        low = (weight - high.astype(F32) - middle.astype(F32)).astype(BF16)
        for step in range(1, CHIPS):
            given(m, step).wait_recv()
        returned = ret[m].reshape(32, width)
        mixed = 0.0
        for piece in (low, middle, high):
            mixed = mixed + lax.dot_general(
                piece, returned, (((0,), (0,)), ((), ())), preferred_element_type=F32
            )
        result = (states[m].astype(F32) + 2.5 * mixed).astype(BF16)
        leaving[m] = result

        @pl.when(section < last)
        def _():
            hop(m).start()

        @pl.when(section == last)
        def _():
            gathered[m, chip] = rms_scale(result, last_gain[...]).astype(BF16)
            for step in (4, 3, 5, 2, 6, 1, 7):
                cast(m, step).start()
            if m == 1:
                for step in range(1, CHIPS):
                    gather(m, step).start()

    @pl.when(section == 0)
    def _():
        head_swap.start()

    def pass_on(m):
        @pl.when(section < last)
        def _():
            cast(m, 1).wait_recv()
            for step in range(1, CHIPS):
                gather(m, step).start()

    lane = iota((8, 128), 1)

    def score(m):
        for step in range(1, CHIPS):
            arriving(m, step).wait_recv()
        if m == 0:
            loads[3].wait()
            head_swap.wait_recv()
        tokens = gathered[m].reshape(CHIPS * tok_count, width)
        target = wanted[m, :, core].reshape(CHIPS * tok_count, 1)
        scores, hits = [], 0.0
        for block, owner in ((head, member), (head_other, partner)):
            logit = lax.dot_general(
                tokens, block[...], (((1,), (1,)), ((), ())), preferred_element_type=F32
            )
            scores.append(logit)
            vocab = iota(logit.shape, 1) + (section * members + owner) * logit.shape[1]
            hits = hits + jnp.sum(jnp.where(vocab == target, logit, 0.0), -1, keepdims=True)
        peak = jnp.max(jnp.maximum(scores[0], scores[1]), -1, keepdims=True)
        total = jnp.sum(jnp.exp(scores[0] - peak) + jnp.exp(scores[1] - peak), -1, keepdims=True)
        spread = iota((CHIPS * tok_count, 128), 1)
        stats = jnp.where(spread == 0, peak, jnp.where(spread == 1, total, jnp.where(spread == 2, hits, 0.0)))
        stat_out[m] = stats.reshape(CHIPS, tok_count, 128)
        for step in range(1, CHIPS):
            stat_to(m, step).start()
        stat_in[m, chip] = stat_out[m, chip]

    def joined(box, m, count):
        pieces = [box[m, k] for k in range(count)]
        peak = pieces[0][:, 0:1]
        for piece in pieces[1:]:
            peak = jnp.maximum(peak, piece[:, 0:1])
        total, hits = 0.0, 0.0
        for piece in pieces:
            total = total + piece[:, 1:2] * jnp.exp(piece[:, 0:1] - peak)
            hits = hits + piece[:, 2:3]
        return peak, total, hits

    def across(m):
        for step in range(1, CHIPS):
            stat_from(m, step).wait_recv()
        peak, total, hits = joined(stat_in, m, CHIPS)
        stats = jnp.where(lane == 0, peak, jnp.where(lane == 1, total, jnp.where(lane == 2, hits, 0.0)))
        plane_out[m] = stats
        for step in range(1, 8):
            plane_to(m, step).start()
        plane_in[m, section] = stats

    pass_on(0)
    score(0)
    pass_on(1)
    across(0)
    score(1)
    across(1)

    sums, counts = 0.0, 0.0
    square = iota((tok_count, tok_count), 0) == iota((tok_count, tok_count), 1)
    for m in range(micro_count):
        for step in range(1, 8):
            plane_from(m, step).wait_recv()
        peak, total, hits = joined(plane_in, m, 8)
        logprob = hits - (peak + jnp.log(total))
        token_out[m : m + 1, :] = jnp.sum(jnp.where(square, logprob, 0.0), 0, keepdims=True)
        sums = sums + jnp.sum(
            jnp.where(lane == own_ids[m, member] + SEQS * m, logprob, 0.0), 0, keepdims=True
        )
        ids = all_ids[m : m + 1, :]
        for k in range(SEQS):
            found = jnp.sum((ids == k).astype(F32), -1, keepdims=True)
            counts = counts + jnp.where(lane[0:1] == SEQS * m + k, found, 0.0)
    seq_out[...] = jnp.broadcast_to(sums, (8, 128))
    for step in range(1, 32):
        seq_to(step).start()
    seq_in[member] = seq_out[...]
    for step in range(1, 32):
        seq_from(step).wait_recv()
    whole = seq_in[0, 0:1, :]
    for k in range(1, 32):
        whole = whole + seq_in[k, 0:1, :]
    mean = whole / jnp.where(counts > 0.0, counts, 1.0)
    mean_out[0:1, :] = mean[:, 0:SEQS]
    mean_out[1:2, :] = mean[:, SEQS : 2 * SEQS]

    head_swap.wait_send()
    for step in range(1, 32):
        seq_to(step).wait_send()
    for m in range(micro_count):
        for step in range(1, CHIPS):
            dispatch(m, step).wait_send()
            giving(m, step).wait_send()
            gather(m, step).wait_send()
            stat_to(m, step).wait_send()
        for step in range(1, 8):
            plane_to(m, step).wait_send()
        pair(m).wait_send()
        halves(m).wait_send()

        @pl.when(section < last)
        def _():
            hop(m).wait_send()

        @pl.when(section == last)
        def _():
            for step in range(1, 8):
                cast(m, step).wait_send()


def body(
    hidden_in, layer_gain, router, w_gate, w_up, w_down, final_gain, head, routing, targets, seq_ids
):
    micro_count, tok_count, width = hidden_in.shape
    sections, members = lax.axis_size("section"), lax.axis_size("expert")
    gate, up, down = w_gate[0], w_up[0], w_down[0]
    vmem, hbm = pl.BlockSpec(memory_space=pltpu.VMEM), pl.BlockSpec(memory_space=pl.ANY)
    block = (micro_count, CHIPS, 2, width)
    dma = pltpu.SemaphoreType.DMA
    own = (micro_count,)
    each = (micro_count, CHIPS)
    return pl.pallas_call(
        layers_kernel,
        out_shape=(
            jax.ShapeDtypeStruct((micro_count, tok_count), F32),
            jax.ShapeDtypeStruct((micro_count, SEQS), F32),
        ),
        in_specs=[vmem] * 8 + [hbm] * 4,
        out_specs=(vmem, vmem),
        scratch_shapes=[
            pltpu.VMEM(gate.shape, BF16),
            pltpu.VMEM(up.shape, BF16),
            pltpu.VMEM(down.shape, BF16),
            pltpu.VMEM(head.shape, BF16),
            pltpu.VMEM(head.shape, BF16),
            pltpu.VMEM((micro_count, CHIPS, tok_count, width), BF16),
            pltpu.VMEM((micro_count, CHIPS, tok_count, 128), F32),
            pltpu.VMEM((micro_count, CHIPS, tok_count, 128), F32),
            pltpu.VMEM((micro_count, tok_count, 128), F32),
            pltpu.VMEM((micro_count, sections, tok_count, 128), F32),
            pltpu.VMEM((8, 128), F32),
            pltpu.VMEM((members, 8, 128), F32),
            pltpu.VMEM(hidden_in.shape, BF16),
            pltpu.VMEM((micro_count, 8, 2, width), BF16),
            pltpu.VMEM(block, BF16),
            pltpu.VMEM(block, BF16),
            pltpu.VMEM((64, width), BF16),
            pltpu.VMEM((64, gate.shape[1]), BF16),
            pltpu.VMEM((32, width), F32),
            pltpu.VMEM(block, BF16),
            pltpu.VMEM(block, BF16),
            pltpu.VMEM(block, BF16),
            pltpu.VMEM(block, BF16),
            pltpu.VMEM(hidden_in.shape, BF16),
            dma((4,)),
            dma(each), dma(each),
            dma(own), dma(own),
            dma(own), dma(own),
            dma(each), dma(each),
            dma(own), dma(own),
            dma, dma,
            dma((micro_count, sections)), dma(own),
            dma(each), dma(each),
            dma(each), dma(each),
            dma((micro_count, sections)), dma((micro_count, sections)),
            dma((members,)), dma((members,)),
        ],
        compiler_params=pltpu.CompilerParams(
            collective_id=0, has_side_effects=True, vmem_limit_bytes=56 << 20
        ),
    )(
        hidden_in, layer_gain, router[0].T, routing[0].transpose(0, 2, 1), final_gain[None],
        targets.reshape(micro_count, CHIPS, 2, tok_count, 1),
        seq_ids.reshape(micro_count, members, tok_count, 1), seq_ids, gate, up, down, head,
    )


def solution(mesh):
    placed = (
        P(None, "expert", None),
        P("section", None),
        P("section", None, None),
        P("section", None, "expert"),
        P("section", None, "expert"),
        P("section", "expert", None),
        P(),
        P(("section", "expert"), None),
        P("section", None, "expert", None),
        P(),
        P(),
    )
    return jax.shard_map(
        body, mesh=mesh, in_specs=placed, out_specs=(P(None, "expert"), P()), check_vma=False
    )
```

time: 628 us -> 237 us (0.38)
  waiting for transfers between devices: 233 us -> 0 us
  Pallas kernels: 0 us -> 229 us
  starting transfers between devices: 123 us -> 0 us
  blocking collectives: 80.7 us -> 0 us
  matrix products: 79.2 us -> 0 us
  other arithmetic: 44.5 us -> 0 us
  local copies, waits for them, and re-layouts: 48.4 us -> 6.91 us
  between operations: 14.2 us -> 0.64 us
    pallas_call x0 -> x1, Pallas kernels: none -> 229 us  [body(): pl.pallas_call(layers_kernel, out_shape=(jax.ShapeDtypeStruct((micro_coun...]
    all_to_all x18 -> x0, waiting for transfers between devices: 169 us -> none  [the longest x9 97.9 us: expert_rows(): lax.all_to_all(partial_value.reshape(sources, slot_count, width_in), EXPE...]
    all_to_all x18 -> x0, starting transfers between devices: 81.3 us -> none  [the longest x9 46.4 us: expert_layer(): lax.all_to_all(outgoing, EXPERT, split_axis=0, concat_axis=0, tiled=True)]
    all_gather x5 -> x0, blocking collectives: 80.7 us -> none  [the longest x4 51.6 us: collected_together(): both, at, found = (lax.all_gather(jnp.concatenate(lines), axis), 0, {})]
    dot_general x37 -> x0, matrix products: 79.2 us -> none  [the longest x9 41.5 us: expert_rows(): jnp.dot(inner, w_down[0], preferred_element_type=jnp.float32)]
    all_gather x1 -> x0, waiting for transfers between devices: 53.5 us -> none  [body(): lax.all_gather(shared, EXPERT, axis=1, tiled=True)]
    ppermute x9 -> x0, starting transfers between devices: 41.3 us -> none  [shifted(): return lax.ppermute(shard, axis, pairs)]
    reduce_sum x57 -> x0, other arithmetic: 22.3 us -> none  [the longest x10 11.7 us: rms_scale(): factor = lax.rsqrt(jnp.mean(values * values, -1, keepdims=True) + 1e-06)]
  transfers between devices with their start and end apart: 28 -> 0, of which waited for: 28 -> 0; matrix products, arithmetic and copies ran while one was open for 4% -> 0% of each run, Pallas kernels for 0% -> 0%
where the time goes in v1:
time: 237 us; the launch traced here: 236 us
  Pallas kernels  229 us (97%)
  local copies, waits for them, and re-layouts  6.91 us (3%)
    pallas_call x1, Pallas kernels, body(): pl.pallas_call(layers_kernel, out_shape=(jax.ShapeDtypeStruct((micro_coun...  229 us

profile of v1, /device:TPU:1, one launch (start us, length us, event | category | flops | bytes accessed | tf_op | source)
XLA Modules:
  0.0 236.4 jit_solution(13825015183887159887)
XLA Ops:
  0.6 1.3 broadcast_in_dim.3.last_gain
  1.9 1.6 reshape.12.wanted
  3.5 1.6 reshape.13.own_ids
  5.1 228.9 %shard_map.122 = (f32[2,8]{1,0:T(2,128)}, f32[2,4]{1,0:T(2,128)}) custom-call(bf16[2,8,3584]{2,1,0:T(8,128)(2,1)} %hidden.1, f32[1,3584]{1,0:T(1,128)} %gain.1, bf16[8,3584]{1,0:T(8,128)(2,1)} %bitcast.12, s32[2,2,8]{2,1,0:T(2,128)} %bitcast.13, f32[1,3584]{1,0:T(1,128)} %broadcast_in_dim.3.last_gain, s32[2,16,2,8,1]{4,3,2,1,0:T(8,128)} %reshape.12.wanted, ...), custom_call_target="tpu_custom_call" | custom-call | tf_op jit(solution)/shard_map/pallas_call | solution.py:400
  234.0 1.2 copy.17
  235.2 1.2 copy.18
